TPU v7x, 32 devices: a whole 2x2x4 slice. The times are simulated.
32 devices in a mesh: dp: 16 (over z, y, x), tensor: 2 (over core).
Axes of the slice: x: 2, y: 2, z: 4, core: 2. Of those that a mesh axis runs over, the one named last changes fastest.
Arguments:
- residual_in: float32 [16, 2048, 640], P('dp'), may hold values from -6 to 6
- cotangent: float32 [16, 2048, 640], P('dp'), may hold values from -6 to 6
- segment_ids: int32 [16, 2048], P('dp'), may hold values from 0 to 15, never falling along the last dimension, each value on 1 to 512 neighbouring positions
- gain_attn_in: float32 [640], replicated, may hold values from 0.25 to 1.75
- w_query: bfloat16 [640, 1024], P(None, 'tensor'), may hold values from -0.25 to 0.25
- w_key: bfloat16 [640, 256], replicated, may hold values from -0.25 to 0.25
- w_value: bfloat16 [640, 256], replicated, may hold values from -0.25 to 0.25
- gain_query: float32 [256], replicated, may hold values from 0.5 to 4
- gain_key: float32 [256], replicated, may hold values from 0.5 to 4
- w_out: bfloat16 [1024, 640], P('tensor'), may hold values from -0.1875 to 0.1875
- gain_attn_out: float32 [640], replicated, may hold values from 0.25 to 1.75
- gain_ff_in: float32 [640], replicated, may hold values from 0.25 to 1.75
- w_gate: bfloat16 [640, 2048], P(None, 'tensor'), may hold values from -0.25 to 0.25
- w_up: bfloat16 [640, 2048], P(None, 'tensor'), may hold values from -0.25 to 0.25
- w_down: bfloat16 [2048, 640], P('tensor'), may hold values from -0.125 to 0.125
- gain_ff_out: float32 [640], replicated, may hold values from 0.25 to 1.75
Outputs:
- output: float32 [16, 2048, 640], P('dp', 'tensor')
- grad_input: float32 [16, 2048, 640], P('dp', 'tensor')
- grad_gain_attn_in: float32 [640], replicated
- grad_w_query: float32 [640, 1024], P(None, ('tensor', 'dp'))
- grad_w_key: float32 [640, 256], replicated
- grad_w_value: float32 [640, 256], replicated
- grad_gain_query: float32 [256], replicated
- grad_gain_key: float32 [256], replicated
- grad_w_out: float32 [1024, 640], P('tensor', 'dp')
- grad_gain_attn_out: float32 [640], replicated
- grad_gain_ff_in: float32 [640], replicated
- grad_w_gate: float32 [640, 2048], P(None, ('tensor', 'dp'))
- grad_w_up: float32 [640, 2048], P(None, ('tensor', 'dp'))
- grad_w_down: float32 [2048, 640], P('tensor', 'dp')
- grad_gain_ff_out: float32 [640], replicated
Inputs may be any that keep to these rules, and one draw needn't show every extreme that they name: `segment_ids`: each row holds 16 sequences numbered from 0 upward in order without gaps; each has 1 to 512 tokens and some sequence of each row has exactly 512.
All inputs are finite; a program needn't handle non-finite values.
Results may differ from a plain program's by a relative error of at most 0.015.
The roundings to bfloat16 on the way count: a program that leaves them out, or rounds other values in their place, can miss the bound.
Values may be sent and summed in bfloat16 or wider, within the bound.
A program may use at most 256 MiB of HBM per device.

v0:
```python
import jax
import jax.numpy as jnp
from jax import lax
from jax.sharding import PartitionSpec as P

D = 640
HEAD_WIDTH = 256
BLOCK = 512
EPS = 1e-06
THETA = 1000000.0
SCORE_SCALE = 0.0625
GELU_C = 0.7978845608028654
GELU_A = 0.044715


def product(left, right):
    return jnp.dot(left, right, preferred_element_type=jnp.float32)


def product_tn(left, right):
    return lax.dot_general(
        left, right, (((0,), (0,)), ((), ())), preferred_element_type=jnp.float32
    )


def product_nt(left, right):
    return lax.dot_general(
        left, right, (((1,), (1,)), ((), ())), preferred_element_type=jnp.float32
    )


def rms_forward(values, gain):
    inv_rms = lax.rsqrt(jnp.mean(values * values, axis=-1, keepdims=True) + EPS)
    normed = values * inv_rms
    return (normed * gain, normed, inv_rms)


def rms_backward(normed, inv_rms, gain, upstream):
    scaled = upstream * gain
    return inv_rms * (scaled - normed * jnp.mean(scaled * normed, axis=-1, keepdims=True))


def positions_of(segment_row):
    token_count = segment_row.shape[0]
    index_row = jnp.arange(token_count, dtype=jnp.int32)
    first_pos = jnp.concatenate([jnp.ones((1,), bool), segment_row[1:] != segment_row[:-1]])
    start_row = lax.cummax(jnp.where(first_pos, index_row, 0), axis=0)
    return index_row - start_row


def rope_tables(positions):
    freq_index = jnp.arange(HEAD_WIDTH // 2, dtype=jnp.float32)
    inv_freq = jnp.exp(freq_index * (-2.0 * jnp.log(THETA) / HEAD_WIDTH))
    angles = positions.astype(jnp.float32)[:, None] * inv_freq[None, :]
    return (jnp.cos(angles)[:, None, :], jnp.sin(angles)[:, None, :])


def rotate(values, cos_tab, sin_tab, direction):
    half_a = values[..., : HEAD_WIDTH // 2]
    half_b = values[..., HEAD_WIDTH // 2 :]
    return jnp.concatenate(
        [
            half_a * cos_tab - direction * half_b * sin_tab,
            half_b * cos_tab + direction * half_a * sin_tab,
        ],
        axis=-1,
    )


def windows(values, front):
    blocks = values.shape[0] // BLOCK
    padded = jnp.concatenate([front, values], axis=0)
    padded = padded.reshape((blocks + 1, BLOCK) + values.shape[1:])
    return jnp.concatenate([padded[:-1], padded[1:]], axis=1)


def window_restore(win_grad):
    own_part = win_grad[:, BLOCK:]
    next_part = jnp.concatenate(
        [win_grad[1:, :BLOCK], jnp.zeros_like(win_grad[:1, :BLOCK])], axis=0
    )
    total = own_part + next_part
    return (total.reshape((total.shape[0] * BLOCK,) + total.shape[2:]), win_grad[0, :BLOCK])


def block_mask(segment_row):
    token_count = segment_row.shape[0]
    blocks = token_count // BLOCK
    index_row = jnp.arange(token_count, dtype=jnp.int32)
    filler = jnp.full((BLOCK,), -1, jnp.int32)
    key_seg = windows(segment_row, filler)
    key_index = windows(index_row, filler)
    query_seg = segment_row.reshape(blocks, BLOCK)
    query_index = index_row.reshape(blocks, BLOCK)
    return (key_seg[:, None, :] == query_seg[:, :, None]) & (
        key_index[:, None, :] <= query_index[:, :, None]
    )


def attn_scores(query_rot, key_rot, key_front, seg_mask):
    token_count, head_total_count = (query_rot.shape[0], query_rot.shape[1])
    blocks = token_count // BLOCK
    query_block = query_rot.reshape(blocks, BLOCK, head_total_count, HEAD_WIDTH)
    key_window = windows(key_rot, key_front)
    logit_scores = (
        jnp.einsum("pjlu,pvu->pljv", query_block, key_window, preferred_element_type=jnp.float32)
        * SCORE_SCALE
    )
    return (jnp.where(seg_mask[:, None], logit_scores, -jnp.inf), query_block, key_window)


def attend_forward(query_rot, key_rot, value_b, key_front, value_front, seg_mask):
    token_count, head_total_count = (query_rot.shape[0], query_rot.shape[1])
    logit_scores, query_block, key_window = attn_scores(query_rot, key_rot, key_front, seg_mask)
    value_window = windows(value_b, value_front)
    row_max = jnp.max(logit_scores, axis=-1, keepdims=True)
    log_total = row_max + jnp.log(jnp.sum(jnp.exp(logit_scores - row_max), axis=-1, keepdims=True))
    attention_weights = jnp.exp(logit_scores - log_total).astype(jnp.bfloat16)
    attention_mixed = jnp.einsum(
        "ipjv,ivx->ijpx", attention_weights, value_window, preferred_element_type=jnp.float32
    )
    return (attention_mixed.reshape(token_count, head_total_count, HEAD_WIDTH), log_total)


def attend_backward(
    query_rot,
    key_rot,
    value_b,
    key_front,
    value_front,
    seg_mask,
    attention_mixed,
    log_total,
    grad_out,
):
    token_count, head_total_count = (query_rot.shape[0], query_rot.shape[1])
    blocks = token_count // BLOCK
    logit_scores, query_block, key_window = attn_scores(query_rot, key_rot, key_front, seg_mask)
    value_window = windows(value_b, value_front)
    attention_weights = jnp.exp(logit_scores - log_total)
    probability_rows = attention_weights.astype(jnp.bfloat16)
    gradient_block = grad_out.reshape(blocks, BLOCK, head_total_count, HEAD_WIDTH)
    probability_gradient = jnp.einsum(
        "pjlu,pvu->pljv", gradient_block, value_window, preferred_element_type=jnp.float32
    )
    row_delta = jnp.sum(grad_out.astype(jnp.float32) * attention_mixed, axis=-1)
    row_delta = row_delta.reshape(blocks, BLOCK, head_total_count).transpose(0, 2, 1)[..., None]
    score_gradient = (attention_weights * (probability_gradient - row_delta) * SCORE_SCALE).astype(
        jnp.bfloat16
    )
    query_gradient = jnp.einsum(
        "ipjv,ivx->ijpx", score_gradient, key_window, preferred_element_type=jnp.float32
    )
    key_gradient, key_back = window_restore(
        jnp.einsum(
            "vptl,vtpm->vlm", score_gradient, query_block, preferred_element_type=jnp.float32
        )
    )
    value_gradient, value_back = window_restore(
        jnp.einsum(
            "vptl,vtpm->vlm", probability_rows, gradient_block, preferred_element_type=jnp.float32
        )
    )
    return (
        query_gradient.reshape(token_count, head_total_count, HEAD_WIDTH),
        key_gradient,
        value_gradient,
        key_back,
        value_back,
    )


def on_device(
    residual_in,
    cotangent,
    segment_ids,
    gain_attn_in,
    w_query,
    w_key,
    w_value,
    gain_query,
    gain_key,
    w_out,
    gain_attn_out,
    gain_ff_in,
    w_gate,
    w_up,
    w_down,
    gain_ff_out,
):
    inputs_all = residual_in[0]
    upstream_all = cotangent[0]
    segment_row = segment_ids[0]
    tok_total = inputs_all.shape[0]
    row_share = tok_total // lax.axis_size("tensor")
    first_row = lax.axis_index("tensor") * row_share

    def own_rows(values):
        return lax.dynamic_slice_in_dim(values, first_row, row_share, 0)

    def mine(values):
        return own_rows(values)

    cos_full, sin_full = rope_tables(positions_of(segment_row))
    mask_full = block_mask(segment_row)
    inputs, upstream, cos_tab, sin_tab, seg_mask = (
        inputs_all,
        upstream_all,
        cos_full,
        sin_full,
        mask_full,
    )
    query_full, gate_full, up_full, out_full, down_full = (w_query, w_gate, w_up, w_out, w_down)
    token_count = inputs.shape[0]
    head_total_count = query_full.shape[1] // HEAD_WIDTH
    normed_in, hat_in, inv_in = rms_forward(inputs, gain_attn_in)
    normed_b = normed_in.astype(jnp.bfloat16)
    query_lin = product(normed_b, query_full).reshape(token_count, head_total_count, HEAD_WIDTH)
    key_lin = product(normed_b, w_key).reshape(token_count, 1, HEAD_WIDTH)
    value_b = product(normed_b, w_value).astype(jnp.bfloat16)
    query_n, query_hat, query_inv = rms_forward(query_lin, gain_query)
    key_n, key_hat, key_inv = rms_forward(key_lin, gain_key)
    query_b = rotate(query_n, cos_tab, sin_tab, 1.0).astype(jnp.bfloat16)
    key_b = rotate(key_n, cos_tab, sin_tab, 1.0).astype(jnp.bfloat16)[:, 0]
    key_front = jnp.zeros((BLOCK, HEAD_WIDTH), jnp.bfloat16)
    value_front = jnp.zeros((BLOCK, HEAD_WIDTH), jnp.bfloat16)
    attention_mixed, log_total = attend_forward(
        query_b, key_b, value_b, key_front, value_front, seg_mask
    )
    attn_flat = attention_mixed.reshape(token_count, head_total_count * HEAD_WIDTH).astype(
        jnp.bfloat16
    )
    attn_part = product(attn_flat, out_full)
    attn_sum = lax.psum(attn_part, "tensor")
    branch_attn, hat_attn, inv_attn = rms_forward(attn_sum, gain_attn_out)
    middle = inputs + branch_attn
    normed_mid, hat_mid, inv_mid = rms_forward(middle, gain_ff_in)
    mid_b = normed_mid.astype(jnp.bfloat16)
    gate_proj = product(mid_b, gate_full)
    up_proj = product(mid_b, up_full)
    tanh_part = jnp.tanh(GELU_C * (gate_proj + GELU_A * gate_proj * gate_proj * gate_proj))
    gelu_val = 0.5 * gate_proj * (1.0 + tanh_part)
    act_b = (gelu_val * up_proj).astype(jnp.bfloat16)
    ff_part = product(act_b, down_full)
    ff_sum = lax.psum(ff_part, "tensor")
    branch_ff, hat_ff, inv_ff = rms_forward(ff_sum, gain_ff_out)
    output = middle + branch_ff
    query_width = query_full.shape[1] // w_query.shape[1]
    unit_width = gate_full.shape[1] // w_gate.shape[1]
    grad_gain_ff_out = jnp.sum(mine(upstream) * mine(hat_ff), axis=0)
    grad_ff = rms_backward(hat_ff, inv_ff, gain_ff_out, upstream).astype(jnp.bfloat16)
    grad_w_down = product_tn(act_b, grad_ff)
    grad_act = product_nt(grad_ff, down_full)
    gelu_deriv = 0.5 * (1.0 + tanh_part) + 0.5 * gate_proj * (
        1.0 - tanh_part * tanh_part
    ) * GELU_C * (1.0 + 3.0 * GELU_A * gate_proj * gate_proj)
    grad_gate = (grad_act * up_proj * gelu_deriv).astype(jnp.bfloat16)
    grad_up = (grad_act * gelu_val).astype(jnp.bfloat16)
    grad_w_gate = product_tn(mid_b, grad_gate).reshape(D, unit_width, -1)
    grad_w_up = product_tn(mid_b, grad_up).reshape(D, unit_width, -1)
    grad_w_down = grad_w_down.reshape(grad_w_down.shape[0], 1, D)
    grad_mid_n = product_nt(grad_gate, gate_full) + product_nt(grad_up, up_full)
    grad_gain_ff_in = jnp.sum(grad_mid_n * hat_mid, axis=0)
    mid_term = rms_backward(hat_mid, inv_mid, gain_ff_in, grad_mid_n)
    grad_middle = upstream + lax.psum(mid_term, "tensor")
    grad_gain_attn_out = jnp.sum(mine(grad_middle) * mine(hat_attn), axis=0)
    grad_attn_sum = rms_backward(hat_attn, inv_attn, gain_attn_out, grad_middle).astype(
        jnp.bfloat16
    )
    grad_w_out = product_tn(attn_flat, grad_attn_sum)
    grad_attn = (
        product_nt(grad_attn_sum, out_full)
        .astype(jnp.bfloat16)
        .reshape(token_count, head_total_count, HEAD_WIDTH)
    )
    key_backs = []
    value_backs = []
    query_gradient, key_gradient, value_gradient, key_back, value_back = attend_backward(
        query_b,
        key_b,
        value_b,
        key_front,
        value_front,
        seg_mask,
        attention_mixed,
        log_total,
        grad_attn,
    )
    key_backs.append(key_back)
    value_backs.append(value_back)
    grad_gain_key = jnp.zeros((HEAD_WIDTH,), jnp.float32)
    key_grad_n = rotate(key_gradient[:, None], cos_tab, sin_tab, -1.0)
    grad_gain_key = grad_gain_key + jnp.sum(key_grad_n * key_hat, axis=(0, 1))
    key_raw = rms_backward(key_hat, key_inv, gain_key, key_grad_n).astype(jnp.bfloat16)[:, 0]
    value_raw = value_gradient.astype(jnp.bfloat16)
    grad_w_key = product_tn(normed_b, key_raw)
    grad_w_value = product_tn(normed_b, value_raw)
    grad_normed = product_nt(key_raw, w_key) + product_nt(value_raw, w_value)
    query_grad_n = rotate(query_gradient, cos_tab, sin_tab, -1.0)
    grad_gain_query = jnp.sum(query_grad_n * query_hat, axis=(0, 1))
    query_raw = (
        rms_backward(query_hat, query_inv, gain_query, query_grad_n)
        .astype(jnp.bfloat16)
        .reshape(token_count, head_total_count * HEAD_WIDTH)
    )
    grad_w_query = product_tn(normed_b, query_raw).reshape(D, query_width, -1)
    grad_w_out = grad_w_out.reshape(grad_w_out.shape[0], 1, D)
    grad_normed = grad_normed + product_nt(query_raw, query_full)
    grad_gain_attn_in = jnp.sum(grad_normed * hat_in, axis=0)
    in_term = rms_backward(hat_in, inv_in, gain_attn_in, grad_normed)
    grad_input = grad_middle + lax.psum(in_term, "tensor")
    share_query, share_out, share_gate, share_up, share_down = (
        lax.psum_scatter(grad_w_query, "dp", scatter_dimension=2, tiled=True),
        lax.psum_scatter(grad_w_out, "dp", scatter_dimension=2, tiled=True),
        lax.psum_scatter(grad_w_gate, "dp", scatter_dimension=2, tiled=True),
        lax.psum_scatter(grad_w_up, "dp", scatter_dimension=2, tiled=True),
        lax.psum_scatter(grad_w_down, "dp", scatter_dimension=2, tiled=True),
    )
    share_query = share_query.reshape(D, -1)
    share_gate = share_gate.reshape(D, -1)
    share_up = share_up.reshape(D, -1)
    share_out = share_out.reshape(share_out.shape[0], -1)
    share_down = share_down.reshape(share_down.shape[0], -1)
    shared_sums = lax.psum(
        (
            grad_gain_attn_in,
            grad_w_key,
            grad_w_value,
            grad_gain_query,
            grad_gain_key,
            grad_gain_attn_out,
            grad_gain_ff_in,
            grad_gain_ff_out,
        ),
        ("dp", "tensor"),
    )
    return (
        mine(output)[None],
        mine(grad_input)[None],
        shared_sums[0],
        share_query,
        shared_sums[1],
        shared_sums[2],
        shared_sums[3],
        shared_sums[4],
        share_out,
        shared_sums[5],
        shared_sums[6],
        share_gate,
        share_up,
        share_down,
        shared_sums[7],
    )


def solution(mesh):
    return jax.shard_map(
        on_device,
        mesh=mesh,
        in_specs=(
            P("dp", None, None),
            P("dp", None, None),
            P("dp", None),
            P(),
            P(None, "tensor"),
            P(),
            P(),
            P(),
            P(),
            P("tensor", None),
            P(),
            P(),
            P(None, "tensor"),
            P(None, "tensor"),
            P("tensor", None),
            P(),
        ),
        out_specs=(
            P("dp", "tensor", None),
            P("dp", "tensor", None),
            P(),
            P(None, ("tensor", "dp")),
            P(),
            P(),
            P(),
            P(),
            P("tensor", "dp"),
            P(),
            P(),
            P(None, ("tensor", "dp")),
            P(None, ("tensor", "dp")),
            P("tensor", "dp"),
            P(),
        ),
        check_vma=False,
    )
```

profile of v0, /device:TPU:0, one launch (start us, length us, event | category | flops | bytes accessed | tf_op | source)
XLA Modules:
  0.0 851.9 jit_solution(15098856227065348030)
XLA Ops:
  10.8 3.0 fusion.12
  14.8 2.0 multiply_convert_fusion.5
  18.8 6.0 broadcast_multiply_fusion.2
  25.1 5.5 fusion.44
  32.2 5.7 multiply_reduce_fusion.11
  41.8 2.6 compare_and_fusion
  44.5 2.4 fusion.51
  48.4 1.9 subtract_convert_fusion
  50.3 5.0 fusion.4
  55.3 3.9 exponential_reduce_fusion
  59.2 1.8 copy-done.11
  61.1 10.4 %bitcast_convert_fusion = (bf16[4,512,2,256]{1,3,2,0:T(8,128)(2,1)}, f32[4,256,2,512]{3,1,2,0:T(8,128)}) fusion(f32[4,1024,512,2]{2,1,3,0:T(8,128)} %copy-done.11, f32[4,2,512]{2,1,0:T(2,128)S(1)} %bitcast.255, pred[4,512,1024]{1,2,0:T(8,128)(4,1)S(1)} %compare_and_fusion, bf16[4,512,256]{1,2,0:T(8,128)(2,1)} %copy.69, bf16[4,512,256]{1,2,0:T(8,128)(2,1)} %copy.68), kind=kOutput, calls=%fused_computation.47 | convolution fusion | flops 2169503744 | bytes 27279360 | tf_op jit(solution)/shard_map/ipjv,ivx->ijpx/dot_general | solution.py:119
  71.5 5.4 copy.74
  78.7 4.2 fusion.60
  82.9 32.5 %all-reduce.20.cloned.1.call-done = f32[2048,640]{1,0:T(8,128)} async-done(((f32[2048,640]{1,0:T(8,128)}), f32[2048,640]{1,0:T(8,128)}) %all-reduce.20.cloned.1.call-update) | async-done | bytes 5242896 | tf_op jit(solution)/shard_map/psum | solution.py:234
  115.4 3.0 multiply_reduce_fusion.8
  119.5 4.8 multiply_reduce_fusion.7
  124.2 2.3 copy-done.3
  127.1 3.4 fusion.61
  130.6 7.2 multiply_convert_fusion.1
  137.7 2.0 copy-done.70
  139.7 5.1 fusion.62
  144.9 30.9 %all-reduce.22.cloned.1.call-done = f32[2048,640]{1,0:T(8,128)} async-done(((f32[2048,640]{1,0:T(8,128)}), f32[2048,640]{1,0:T(8,128)}) %all-reduce.22.cloned.1.call-update) | async-done | bytes 5242896 | tf_op jit(solution)/shard_map/psum | solution.py:245
  175.9 3.0 multiply_reduce_fusion.6
  179.0 4.9 multiply_reduce_fusion.5
  186.5 15.7 %multiply_convert_fusion = (bf16[2048,1024]{1,0:T(8,128)(2,1)}, bf16[2048,1024]{1,0:T(8,128)(2,1)}) fusion(f32[2048,1024]{1,0:T(8,128)} %copy-done.71, f32[2048,1024]{1,0:T(8,128)} %get-tuple-element.99, bf16[2048,640]{1,0:T(8,128)(2,1)S(1)} %multiply_convert_fusion.3, bf16[1024,640]{1,0:T(8,128)(2,1)S(1)} %copy-done.66), kind=kOutput, calls=%fused_computation.18 | convolution fusion | flops 2732589056 | bytes 29097984 | tf_op jit(solution)/shard_map/dot_general | solution.py:27
  202.2 5.3 fusion.63
  207.5 6.1 multiply_reduce_fusion
  213.7 2.9 subtract_multiply_fusion.1
  216.7 30.9 %all-reduce.24.cloned.1.call-done = f32[2048,640]{1,0:T(8,128)} async-done(((f32[2048,640]{1,0:T(8,128)}), f32[2048,640]{1,0:T(8,128)}) %all-reduce.24.cloned.1.call-update) | async-done | bytes 5242896 | tf_op jit(solution)/shard_map/psum | solution.py:265
  247.6 6.5 multiply_reduce_fusion.3
  258.0 1.8 convolution_convert_fusion
  259.8 2.1 reshape_reshape.4
  261.9 4.7 copy.77
  266.7 3.7 fusion.13
  270.8 12.1 %fusion.2 = bf16[4,2,512,1024]{2,3,1,0:T(8,128)(2,1)} fusion(f32[4,1024,512,2]{2,1,3,0:T(8,128)} %copy-done.11, bf16[4,512,2,256]{1,3,2,0:T(8,128)(2,1)S(1)} %copy.77, f32[4,2,512]{2,1,0:T(2,128)S(1)} %bitcast.254, f32[4,2,512]{2,1,0:T(2,128)S(1)} %bitcast.256, pred[4,512,1024]{1,2,0:T(8,128)(4,1)S(1)} %copy-done.16, ...), kind=kOutput, calls=%fused_computation.3 | convolution fusion | flops 2181038080 | bytes 31490048 | tf_op jit(solution)/shard_map/pjlu,pvu->pljv/dot_general | solution.py:143
  283.0 8.2 convolution_bitcast_fusion
  291.2 7.9 convolution_bitcast_fusion.2
  299.1 8.4 convolution_bitcast_fusion.1
  307.5 5.5 copy.81
  313.0 2.8 multiply_subtract_fusion
  318.2 2.7 multiply_convert_fusion.7
  320.8 3.0 copy.82
  323.9 1.9 fusion.65
  326.7 4.5 fusion.48
  337.1 2.6 multiply_reduce_fusion.1
  339.7 2.9 subtract_multiply_fusion
  342.7 7.4 convolution_bitcast_fusion.5
  350.1 6.8 copy.85
  356.9 7.5 convolution_bitcast_fusion.4
  364.4 6.7 copy.86
  371.2 8.3 convolution_bitcast_fusion.3
  379.5 6.5 copy.87
  386.0 3.3 fusion.39
  389.3 2.1 copy.83
  391.4 4.2 convolution_bitcast_fusion.6
  395.6 2.1 copy.84
  401.0 5.4 fusion.16
  410.0 5.3 multiply_reduce_fusion.12
  415.3 44.3 %all-reduce.10 = (f32[640]{0:T(1024)}, f32[256]{0:T(256)}, f32[256]{0:T(256)}, f32[640]{0:T(1024)}, f32[640]{0:T(1024)}, /*index=5*/f32[640]{0:T(1024)}) all-reduce(f32[640]{0:T(1024)S(1)} %get-tuple-element.47, f32[256]{0:T(256)S(1)} %get-tuple-element.49, ...), channel_id=1, replica_groups=mesh['dp'=16,'tensor'=2] {'dp','tensor'}, use_global_device_ids=true, to_apply=%region_22.23 | all-reduce | flops 3072 | bytes 24576 | tf_op jit(solution)/shard_map/psum | solution.py:324
  459.6 244.1 %all-reduce.30.cloned.1.call-done = (f32[640,1,512]{0,1,2:T(1,128)}, f32[512,1,640]{0,1,2:T(1,128)}, f32[640,1,1024]{0,1,2:T(1,128)}, f32[640,1,1024]{0,1,2:T(1,128)}, f32[1024,1,640]{0,1,2:T(1,128)}) async-done(((f32[640,1,512]{0,1,2:T(1,128)}, f32[512,1,640]{0,1,2:T(1,128)}, f32[640,1,1024]{0,1,2:T(1,128)}, f32[640,1,1024]{0,1,2:T(1,128)}, f32[1024,1,640]{0,1,2:T(1,128)}), (f32[640,1,512]{0,1,2:T(1,128)}, ...) | async-done | bytes 10485776
  711.7 129.2 %all-reduce.28.cloned.1.call-done = (f32[640,256]{1,0:T(8,128)}, f32[640,256]{1,0:T(8,128)}) async-done(((f32[640,256]{1,0:T(8,128)}, f32[640,256]{1,0:T(8,128)}), (f32[640,256]{1,0:T(8,128)}, f32[640,256]{1,0:T(8,128)})) %all-reduce.28.cloned.1.call-update) | async-done | bytes 1310736 | tf_op jit(solution)/shard_map/psum | solution.py:324
  840.9 2.0 copy.135
  842.9 2.0 copy.136
  (249 shorter events, 45.8 us)
Async XLA Ops:
  7.2 123.4 %copy-start = (bf16[640,1024]{1,0:T(8,128)(2,1)S(1)}, bf16[640,1024]{1,0:T(8,128)(2,1)}, u32[]{:S(2)}) copy-start(bf16[640,1024]{1,0:T(8,128)(2,1)} %param.29) | copy-start | bytes 3932164
  7.2 6.7 copy-start.52
  7.2 108.2 %all-reduce.20.cloned.1.call-start = ((), (), s32[]{:S(2)}) async-start(), calls=%async_computation | async-start | bytes 10485760 | tf_op jit(solution)/shard_map/psum | solution.py:234
  7.3 17.8 %copy-start.63 = (f32[128]{0:T(128)}, f32[128]{0:T(128)S(1)}, u32[]{:S(2)}) copy-start(f32[128]{0:T(128)S(1)} %multiply_exponential_fusion) | copy-start | bytes 1540
  10.8 4.0 copy-start.2
  14.8 23.1 %copy-start.44 = (f32[2048]{0:T(1024)}, f32[2048]{0:T(1024)S(1)}, u32[]{:S(2)}) copy-start(f32[2048]{0:T(1024)S(1)} %add_rsqrt_fusion.5) | copy-start | bytes 24580
  16.9 7.9 copy-start.60
  18.1 12.6 %copy-start.6 = (f32[2048,256]{1,0:T(8,128)}, f32[2048,256]{1,0:T(8,128)S(1)}, u32[]{:S(2)}) copy-start(f32[2048,256]{1,0:T(8,128)S(1)} %get-tuple-element.93) | copy-start | bytes 6291460
  18.1 12.6 %copy-start.48 = (f32[2048]{0:T(1024)}, f32[2048]{0:T(1024)S(1)}, u32[]{:S(2)}) copy-start(f32[2048]{0:T(1024)S(1)} %add_rsqrt_fusion.4) | copy-start | bytes 24580
  18.8 11.9 %copy-start.50 = (f32[2048]{0:T(1024)}, f32[2048]{0:T(1024)S(1)}, u32[]{:S(2)}) copy-start(f32[2048]{0:T(1024)S(1)} %fusion.52) | copy-start | bytes 24580
  30.7 7.3 slice-start
  32.1 5.8 slice-start.1
  32.2 5.8 copy-start.36
  38.0 8.9 %copy-start.46 = (f32[2048,2]{0,1:T(2,128)}, f32[2048,2]{0,1:T(2,128)S(1)}, u32[]{:S(2)}) copy-start(f32[2048,2]{0,1:T(2,128)S(1)} %add_rsqrt_fusion) | copy-start | bytes 49156
  39.1 7.7 copy-start.58
  40.5 4.0 copy-start.31
  41.8 5.1 copy-start.4
  44.5 16.6 %copy-start.15 = (pred[4,512,1024]{1,2,0:T(8,128)(4,1)}, pred[4,512,1024]{1,2,0:T(8,128)(4,1)S(1)}, u32[]{:S(2)}) copy-start(pred[4,512,1024]{1,2,0:T(8,128)(4,1)S(1)} %compare_and_fusion) | copy-start | bytes 6291460
  55.3 5.8 copy-start.11
  82.9 35.6 %copy-start.56 = (f32[640]{0:T(1024)S(1)}, f32[640]{0:T(1024)}, u32[]{:S(2)}) copy-start(f32[640]{0:T(1024)} %param.26) | copy-start | bytes 7684
  82.9 93.0 %all-reduce.22.cloned.1.call-start = ((), (), s32[]{:S(2)}) async-start(), calls=%async_computation.1 | async-start | bytes 10485760 | tf_op jit(solution)/shard_map/psum | solution.py:245
  115.4 4.0 copy-start.10
  119.5 7.1 copy-start.57
  127.1 3.5 copy-start.27
  130.5 7.2 copy-start.71
  130.6 9.2 %copy-start.65 = (bf16[1024,640]{1,0:T(8,128)(2,1)S(1)}, bf16[1024,640]{1,0:T(8,128)(2,1)}, u32[]{:S(2)}) copy-start(bf16[1024,640]{1,0:T(8,128)(2,1)} %param.30) | copy-start | bytes 3932164
  144.9 34.1 %copy-start.54 = (f32[640]{0:T(1024)S(1)}, f32[640]{0:T(1024)}, u32[]{:S(2)}) copy-start(f32[640]{0:T(1024)} %param.31) | copy-start | bytes 7684
  144.9 102.7 %all-reduce.24.cloned.1.call-start = ((), (), s32[]{:S(2)}) async-start(), calls=%async_computation.2 | async-start | bytes 10485760 | tf_op jit(solution)/shard_map/psum | solution.py:265
  175.9 8.0 slice-start.4
  178.9 5.0 slice-start.5
  183.9 23.6 %slice-start.6 = ((s8[5242880]{0:T(1024)(128)(4,1)}), s8[4194304]{0:T(1024)(128)(4,1)S(1)}, s32[]{:S(2)}) async-start(s8[5242880]{0:T(1024)(128)(4,1)} %bitcast.215), calls=%async_computation.12 | async-start | bytes 8388608
  186.5 15.7 %copy-start.28 = (bf16[2048,640]{1,0:T(8,128)(2,1)}, bf16[2048,640]{1,0:T(8,128)(2,1)S(1)}, u32[]{:S(2)}) copy-start(bf16[2048,640]{1,0:T(8,128)(2,1)S(1)} %multiply_convert_fusion.3) | copy-start | bytes 7864324
  186.5 15.7 %copy-start.68 = (bf16[640,1024]{1,0:T(8,128)(2,1)S(1)}, bf16[640,1024]{1,0:T(8,128)(2,1)}, u32[]{:S(2)}) copy-start(bf16[640,1024]{1,0:T(8,128)(2,1)} %param.28) | copy-start | bytes 3932164
  186.5 21.0 %slice-start.7 = ((s8[5242880]{0:T(1024)(128)(4,1)}), s8[1048576]{0:T(1024)(128)(4,1)S(1)}, s32[]{:S(2)}) async-start(s8[5242880]{0:T(1024)(128)(4,1)} %bitcast.215), calls=%async_computation.13 | async-start | bytes 2097152
  216.6 37.5 %slice-start.8 = ((s8[5242880]{0:T(1024)(128)(4,1)}), s8[1048576]{0:T(1024)(128)(4,1)S(1)}, s32[]{:S(2)}) async-start(s8[5242880]{0:T(1024)(128)(4,1)} %bitcast.217), calls=%async_computation.14 | async-start | bytes 2097152
  216.6 193.3 %all-reduce.26.cloned.1.call-start = ((), (), s32[]{:S(2)}) async-start(), calls=%async_computation.3 | async-start | bytes 10485760 | tf_op jit(solution)/shard_map/psum | solution.py:311
  247.6 6.7 slice-start.9
  254.3 3.7 copy-start.43
  266.6 16.3 %copy-start.17 = (bf16[4,512,2,256]{1,3,2,0:T(8,128)(2,1)}, bf16[4,512,2,256]{1,3,2,0:T(8,128)(2,1)S(1)}, u32[]{:S(2)}) copy-start(bf16[4,512,2,256]{1,3,2,0:T(8,128)(2,1)S(1)} %copy.77) | copy-start | bytes 6291460
  266.6 3.7 copy-start.16
  266.6 3.9 copy-start.38
  266.7 4.2 copy-start.39
  270.8 12.1 %copy-start.32 = (bf16[2048,1,128]{2,0,1:T(8,128)(2,1)S(1)}, bf16[2048,1,128]{2,0,1:T(8,128)(2,1)}, u32[]{:S(2)}) copy-start(bf16[2048,1,128]{2,0,1:T(8,128)(2,1)} %get-tuple-element.85) | copy-start | bytes 1572868
  270.8 12.1 %copy-start.33 = (bf16[2048,1,128]{2,0,1:T(8,128)(2,1)S(1)}, bf16[2048,1,128]{2,0,1:T(8,128)(2,1)}, u32[]{:S(2)}) copy-start(bf16[2048,1,128]{2,0,1:T(8,128)(2,1)} %get-tuple-element.86) | copy-start | bytes 1572868
  283.0 8.2 copy-start.40
  283.0 8.2 copy-start.41
  283.0 16.1 %slice-start.10 = ((s8[16777216]{0:T(1024)(128)(4,1)}), s8[4194304]{0:T(1024)(128)(4,1)S(1)}, s32[]{:S(2)}) async-start(s8[16777216]{0:T(1024)(128)(4,1)} %bitcast.219), calls=%async_computation.16 | async-start | bytes 8388608
  283.0 16.1 %slice-start.11 = ((s8[16777216]{0:T(1024)(128)(4,1)}), s8[4194304]{0:T(1024)(128)(4,1)S(1)}, s32[]{:S(2)}) async-start(s8[16777216]{0:T(1024)(128)(4,1)} %bitcast.219), calls=%async_computation.17 | async-start | bytes 8388608
  291.2 7.9 slice-start.12
  291.2 7.9 slice-start.13
  307.5 5.5 copy-start.14
  307.5 5.5 copy-start.20
  313.0 3.5 copy-start.5
  313.0 3.4 copy-start.47
  313.0 3.4 copy-start.59
  326.2 5.1 copy-start.7
  326.2 5.1 copy-start.49
  326.2 5.1 copy-start.61
  331.3 5.1 slice-start.2
  342.7 361.0 %all-reduce.30.cloned.1.call-start = ((), (), s32[]{:S(2)}) async-start(), calls=%async_computation.5 | async-start | bytes 20971520
  397.8 443.1 %all-reduce.28.cloned.1.call-start = ((), (), s32[]{:S(2)}) async-start(), calls=%async_computation.4 | async-start | bytes 2621440 | tf_op jit(solution)/shard_map/psum | solution.py:324
  401.0 5.5 copy-start.19
  401.0 5.5 copy-start.26
  410.0 434.9 %copy-start.1 = (bf16[640,1024]{1,0:T(8,128)(2,1)S(1)}, bf16[640,1024]{1,0:T(8,128)(2,1)}, u32[]{:S(2)}) copy-start(bf16[640,1024]{1,0:T(8,128)(2,1)} %param.29) | copy-start | bytes 3932164
  (28 other events, 55.3 us)
Sparse Core Ops, SparseCore 0:
  83.0 32.3 all-reduce.19
  145.0 30.8 all-reduce.21
  216.8 30.8 all-reduce.23
  342.8 30.8 all-reduce.25
  397.9 305.7 all-reduce.29
  709.7 131.2 all-reduce.27
where the time goes:
time: 856 us; the launch traced here: 852 us
  waiting for transfers between devices  468 us (55%)
  matrix products  148 us (17%)
  other arithmetic  90.9 us (11%)
  local copies, waits for them, and re-layouts  82.6 us (10%)
  blocking collectives  44.3 us (5%)
  between operations  17.4 us (2%)
    unnamed x7, waiting for transfers between devices  244 us
    psum x1, waiting for transfers between devices, on_device(): lax.psum((grad_gain_attn_in, grad_w_key, grad_w_value, grad_gain_query, g...  129 us
    psum x1, blocking collectives, on_device(): lax.psum((grad_gain_attn_in, grad_w_key, grad_w_value, grad_gain_query, g...  44.3 us
    dot_general x7, matrix products, product_nt(): lax.dot_general(left, right, (((1,), (1,)), ((), ())), preferred_element_...  34.4 us
    dot_general x7, matrix products, product_tn(): lax.dot_general(left, right, (((0,), (0,)), ((), ())), preferred_element_...  34.2 us
    psum x1, waiting for transfers between devices, on_device(): attn_sum = lax.psum(attn_part, 'tensor')  32.5 us
    unnamed x187, local copies, waits for them, and re-layouts  32.3 us
    psum x1, waiting for transfers between devices, on_device(): grad_middle = upstream + lax.psum(mid_term, 'tensor')  30.9 us
  transfers between devices with their start and end apart: 6, of which 5 were waited for; matrix products, arithmetic and copies ran while one was open for 9% of the time, Pallas kernels for 0%

commit v1 on v0

--- a/solution.py
+++ b/solution.py
@@ -321,19 +321,18 @@
     share_up = share_up.reshape(D, -1)
     share_out = share_out.reshape(share_out.shape[0], -1)
     share_down = share_down.reshape(share_down.shape[0], -1)
-    shared_sums = lax.psum(
-        (
-            grad_gain_attn_in,
-            grad_w_key,
-            grad_w_value,
-            grad_gain_query,
-            grad_gain_key,
-            grad_gain_attn_out,
-            grad_gain_ff_in,
-            grad_gain_ff_out,
-        ),
-        ("dp", "tensor"),
-    )
+    shared_sums = (
+        grad_gain_attn_in,
+        grad_w_key,
+        grad_w_value,
+        grad_gain_query,
+        grad_gain_key,
+        grad_gain_attn_out,
+        grad_gain_ff_in,
+        grad_gain_ff_out,
+    )
+    for d in ("tensor", "dp"):
+        shared_sums = lax.psum(shared_sums, d)
     return (
         mine(output)[None],
         mine(grad_input)[None],

time: 856 us -> 770 us (0.90)
  waiting for transfers between devices: 468 us -> 337 us
  blocking collectives: 44.3 us -> 85.5 us
    psum x1 -> x0, waiting for transfers between devices: 129 us -> none  [on_device(): lax.psum((grad_gain_attn_in, grad_w_key, grad_w_value, grad_gain_query, g...]
    psum x1 -> x2, blocking collectives: 44.3 us -> 85.5 us  [on_device(): shared_sums = lax.psum(shared_sums, d)]
    unnamed x7 -> x6, waiting for transfers between devices: 244 us -> 243 us
  transfers between devices with their start and end apart: 6 -> 5, of which waited for: 5 -> 4; matrix products, arithmetic and copies ran while one was open for 9% -> 9% of each run, Pallas kernels for 0% -> 0%
where the time goes in v1:
time: 770 us; the launch traced here: 766 us
  waiting for transfers between devices  337 us (44%)
  matrix products  151 us (20%)
  other arithmetic  91.8 us (12%)
  blocking collectives  85.5 us (11%)
  local copies, waits for them, and re-layouts  83.1 us (11%)
  between operations  17.1 us (2%)
    unnamed x6, waiting for transfers between devices  243 us
    psum x2, blocking collectives, on_device(): shared_sums = lax.psum(shared_sums, d)  85.5 us
    dot_general x7, matrix products, product_nt(): lax.dot_general(left, right, (((1,), (1,)), ((), ())), preferred_element_...  36.7 us
    dot_general x7, matrix products, product_tn(): lax.dot_general(left, right, (((0,), (0,)), ((), ())), preferred_element_...  34.9 us
    psum x1, waiting for transfers between devices, on_device(): attn_sum = lax.psum(attn_part, 'tensor')  32.5 us
    unnamed x187, local copies, waits for them, and re-layouts  31.6 us
    psum x1, waiting for transfers between devices, on_device(): grad_middle = upstream + lax.psum(mid_term, 'tensor')  30.9 us
    psum x1, waiting for transfers between devices, on_device(): ff_sum = lax.psum(ff_part, 'tensor')  30.9 us
  transfers between devices with their start and end apart: 5, of which 4 were waited for; matrix products, arithmetic and copies ran while one was open for 9% of the time, Pallas kernels for 0%

profile of v1, /device:TPU:0, one launch (start us, length us, event | category | flops | bytes accessed | tf_op | source)
XLA Modules:
  0.0 766.3 jit_solution(8173294327079431604)
XLA Ops:
  10.8 3.0 fusion.12
  14.8 2.0 multiply_convert_fusion.5
  18.8 6.2 broadcast_multiply_fusion.2
  25.3 5.5 fusion.44
  32.3 5.7 multiply_reduce_fusion.11
  42.0 2.6 compare_and_fusion
  44.7 2.4 fusion.51
  48.6 1.9 subtract_convert_fusion
  50.5 5.0 fusion.4
  55.5 3.9 exponential_reduce_fusion
  59.4 1.8 copy-done.11
  61.3 10.4 %bitcast_convert_fusion = (bf16[4,512,2,256]{1,3,2,0:T(8,128)(2,1)}, f32[4,256,2,512]{3,1,2,0:T(8,128)}) fusion(f32[4,1024,512,2]{2,1,3,0:T(8,128)} %copy-done.11, f32[4,2,512]{2,1,0:T(2,128)S(1)} %bitcast.257, pred[4,512,1024]{1,2,0:T(8,128)(4,1)S(1)} %compare_and_fusion, bf16[4,512,256]{1,2,0:T(8,128)(2,1)} %copy.69, bf16[4,512,256]{1,2,0:T(8,128)(2,1)} %copy.68), kind=kOutput, calls=%fused_computation.47 | convolution fusion | flops 2169503744 | bytes 27279360 | tf_op jit(solution)/shard_map/ipjv,ivx->ijpx/dot_general | solution.py:119
  71.7 5.0 copy.74
  78.5 4.2 fusion.60
  82.8 32.5 %all-reduce.20.cloned.1.call-done = f32[2048,640]{1,0:T(8,128)} async-done(((f32[2048,640]{1,0:T(8,128)}), f32[2048,640]{1,0:T(8,128)}) %all-reduce.20.cloned.1.call-update) | async-done | bytes 5242896 | tf_op jit(solution)/shard_map/psum | solution.py:234
  115.3 3.0 multiply_reduce_fusion.8
  119.3 4.8 multiply_reduce_fusion.7
  124.1 2.3 copy-done.3
  126.9 3.4 fusion.61
  130.4 7.2 multiply_convert_fusion.1
  137.6 2.0 copy-done.68
  139.6 5.1 fusion.62
  144.8 30.9 %all-reduce.22.cloned.1.call-done = f32[2048,640]{1,0:T(8,128)} async-done(((f32[2048,640]{1,0:T(8,128)}), f32[2048,640]{1,0:T(8,128)}) %all-reduce.22.cloned.1.call-update) | async-done | bytes 5242896 | tf_op jit(solution)/shard_map/psum | solution.py:245
  175.7 3.0 multiply_reduce_fusion.6
  178.8 4.9 multiply_reduce_fusion.5
  186.4 15.7 %multiply_convert_fusion = (bf16[2048,1024]{1,0:T(8,128)(2,1)}, bf16[2048,1024]{1,0:T(8,128)(2,1)}) fusion(f32[2048,1024]{1,0:T(8,128)} %copy-done.69, f32[2048,1024]{1,0:T(8,128)} %get-tuple-element.108, bf16[2048,640]{1,0:T(8,128)(2,1)S(1)} %multiply_convert_fusion.3, bf16[1024,640]{1,0:T(8,128)(2,1)S(1)} %copy-done.64), kind=kOutput, calls=%fused_computation.18 | convolution fusion | flops 2732589056 | bytes 29097984 | tf_op jit(solution)/shard_map/dot_general | solution.py:27
  202.1 5.3 fusion.63
  207.4 6.1 multiply_reduce_fusion
  213.5 2.9 subtract_multiply_fusion.1
  216.5 30.9 %all-reduce.24.cloned.1.call-done = f32[2048,640]{1,0:T(8,128)} async-done(((f32[2048,640]{1,0:T(8,128)}), f32[2048,640]{1,0:T(8,128)}) %all-reduce.24.cloned.1.call-update) | async-done | bytes 5242896 | tf_op jit(solution)/shard_map/psum | solution.py:265
  247.5 6.5 multiply_reduce_fusion.3
  259.7 2.1 reshape_reshape.4
  261.8 4.7 copy.77
  266.5 3.7 fusion.13
  270.7 12.1 %fusion.2 = bf16[4,2,512,1024]{2,3,1,0:T(8,128)(2,1)} fusion(f32[4,1024,512,2]{2,1,3,0:T(8,128)} %copy-done.11, bf16[4,512,2,256]{1,3,2,0:T(8,128)(2,1)S(1)} %copy.77, f32[4,2,512]{2,1,0:T(2,128)S(1)} %bitcast.256, f32[4,2,512]{2,1,0:T(2,128)S(1)} %bitcast.258, pred[4,512,1024]{1,2,0:T(8,128)(4,1)S(1)} %copy-done.16, ...), kind=kOutput, calls=%fused_computation.3 | convolution fusion | flops 2181038080 | bytes 31490048 | tf_op jit(solution)/shard_map/pjlu,pvu->pljv/dot_general | solution.py:143
  282.9 8.2 %convolution_bitcast_fusion = f32[4,512,2,256]{1,3,2,0:T(8,128)} fusion(bf16[4,2,512,1024]{2,3,1,0:T(8,128)(2,1)} %fusion.2, bf16[4,512,128]{2,1,0:T(8,128)(2,1)S(1)} %bitcast.240, bf16[4,512,128]{2,1,0:T(8,128)(2,1)S(1)} %bitcast.237, bf16[4,512,256]{2,1,0:T(8,128)(2,1)} %bitcast.242), kind=kOutput, calls=%fused_computation.74 | convolution fusion | flops 2153775104 | bytes 14680064 | tf_op jit(solution)/shard_map/ipjv,ivx->ijpx/dot_general | solution.py:151
  291.1 7.9 %convolution_bitcast_fusion.2 = f32[4,1024,256]{2,1,0:T(8,128)} fusion(bf16[4,2,512,1024]{2,3,1,0:T(8,128)(2,1)} %fusion.2, bf16[4,512,2,128]{3,1,0,2:T(8,128)(2,1)S(1)} %bitcast.246, bf16[4,512,2,128]{3,1,0,2:T(8,128)(2,1)S(1)} %bitcast.244), kind=kOutput, calls=%fused_computation.76 | convolution fusion | flops 2151677952 | bytes 14680064 | tf_op jit(solution)/shard_map/vptl,vtpm->vlm/dot_general | solution.py:155
  299.0 8.3 %convolution_bitcast_fusion.1 = f32[4,1024,256]{2,1,0:T(8,128)} fusion(bf16[4,512,2,256]{1,3,2,0:T(8,128)(2,1)} %copy-done.17, f32[4,1024,512,2]{2,1,3,0:T(8,128)S(1)} %bitcast.222, f32[4,2,512]{2,1,0:T(2,128)S(1)} %bitcast.259, pred[4,512,1024]{1,2,0:T(8,128)(4,1)} %copy-done.15), kind=kOutput, calls=%fused_computation.75 | convolution fusion | flops 2164260864 | bytes 25182208 | tf_op jit(solution)/shard_map/vptl,vtpm->vlm/dot_general | solution.py:160
  308.9 2.0 slice_add_fusion.1
  310.9 4.6 fusion.48
  317.1 3.4 fusion.64
  322.2 5.4 copy.81
  327.6 2.8 multiply_subtract_fusion
  332.8 2.7 multiply_convert_fusion.7
  335.4 3.2 copy.82
  338.7 1.9 fusion.65
  345.0 2.6 multiply_reduce_fusion.1
  347.6 2.9 subtract_multiply_fusion
  350.6 7.4 convolution_bitcast_fusion.5
  358.0 6.9 copy.85
  364.9 7.5 convolution_bitcast_fusion.4
  372.4 6.6 copy.86
  379.1 9.1 %convolution_bitcast_fusion.3 = f32[1024,1,640]{2,0,1:T(8,128)} fusion(bf16[2048,1024]{1,0:T(8,128)(2,1)} %copy-done.68, bf16[2048,640]{1,0:T(8,128)(2,1)} %copy-done.24), kind=kOutput, calls=%fused_computation.99 | convolution fusion | flops 2684354560 | bytes 9437184 | tf_op jit(solution)/shard_map/dot_general | solution.py:21
  388.2 6.5 copy.87
  394.7 3.3 fusion.39
  398.0 2.1 copy.83
  400.1 4.2 convolution_bitcast_fusion.6
  404.3 2.2 copy.84
  409.7 5.3 fusion.16
  415.8 4.6 multiply_reduce_fusion.12
  420.5 3.7 all-reduce.12
  424.2 81.8 %all-reduce.10 = (f32[640]{0:T(1024)}, f32[256]{0:T(256)}, f32[256]{0:T(256)}, f32[640]{0:T(1024)}, f32[640]{0:T(1024)}, /*index=5*/f32[640]{0:T(1024)}) all-reduce(f32[640]{0:T(1024)S(1)} %get-tuple-element.66, f32[256]{0:T(256)S(1)} %get-tuple-element.67, ...), channel_id=1, replica_groups=mesh['dp'=16,'tensor'=2] {'dp'}, use_global_device_ids=true, to_apply=%region_23.24 | all-reduce | flops 3072 | bytes 24576 | tf_op jit(solution)/shard_map/psum | solution.py:335
  506.0 242.7 %all-reduce.26.cloned.1.call-done = (f32[640,1,512]{0,1,2:T(1,128)}, f32[640,256]{1,0:T(8,128)}, f32[640,256]{1,0:T(8,128)}, f32[512,1,640]{0,1,2:T(1,128)}, f32...) async-done(((f32[640,1,512]{0,1,2:T(1,128)}, f32[640,256]{1,0:T(8,128)}, f32[640,256]{1,0:T(8,128)}, f32[512,1,640]{0,1,2:T(1,128)}, ...) | async-done | bytes 11796496
  756.7 2.0 copy.137
  (248 shorter events, 48.4 us)
Async XLA Ops:
  7.2 123.2 %copy-start = (bf16[640,1024]{1,0:T(8,128)(2,1)S(1)}, bf16[640,1024]{1,0:T(8,128)(2,1)}, u32[]{:S(2)}) copy-start(bf16[640,1024]{1,0:T(8,128)(2,1)} %param.29) | copy-start | bytes 3932164
  7.2 6.7 copy-start.50
  7.2 108.0 %all-reduce.20.cloned.1.call-start = ((), (), s32[]{:S(2)}) async-start(), calls=%async_computation | async-start | bytes 10485760 | tf_op jit(solution)/shard_map/psum | solution.py:234
  7.3 18.0 %copy-start.61 = (f32[128]{0:T(128)}, f32[128]{0:T(128)S(1)}, u32[]{:S(2)}) copy-start(f32[128]{0:T(128)S(1)} %multiply_exponential_fusion) | copy-start | bytes 1540
  10.8 4.0 copy-start.2
  14.8 23.3 %copy-start.42 = (f32[2048]{0:T(1024)}, f32[2048]{0:T(1024)S(1)}, u32[]{:S(2)}) copy-start(f32[2048]{0:T(1024)S(1)} %add_rsqrt_fusion.5) | copy-start | bytes 24580
  16.9 8.1 %copy-start.56 = (f32[256]{0:T(256)S(1)}, f32[256]{0:T(256)}, u32[]{:S(2)}) copy-start(f32[256]{0:T(256)} %param.24) | copy-start | bytes 3076
  18.1 12.8 %copy-start.6 = (f32[2048,256]{1,0:T(8,128)}, f32[2048,256]{1,0:T(8,128)S(1)}, u32[]{:S(2)}) copy-start(f32[2048,256]{1,0:T(8,128)S(1)} %get-tuple-element.102) | copy-start | bytes 6291460
  18.1 12.7 %copy-start.46 = (f32[2048]{0:T(1024)}, f32[2048]{0:T(1024)S(1)}, u32[]{:S(2)}) copy-start(f32[2048]{0:T(1024)S(1)} %add_rsqrt_fusion.4) | copy-start | bytes 24580
  18.8 12.1 %copy-start.48 = (f32[2048]{0:T(1024)}, f32[2048]{0:T(1024)S(1)}, u32[]{:S(2)}) copy-start(f32[2048]{0:T(1024)S(1)} %fusion.52) | copy-start | bytes 24580
  30.8 7.3 slice-start
  32.3 5.8 slice-start.1
  32.3 5.8 copy-start.33
  38.2 8.9 %copy-start.44 = (f32[2048,2]{0,1:T(2,128)}, f32[2048,2]{0,1:T(2,128)S(1)}, u32[]{:S(2)}) copy-start(f32[2048,2]{0,1:T(2,128)S(1)} %add_rsqrt_fusion) | copy-start | bytes 49156
  39.3 7.8 %copy-start.58 = (f32[256]{0:T(256)S(1)}, f32[256]{0:T(256)}, u32[]{:S(2)}) copy-start(f32[256]{0:T(256)} %param.23) | copy-start | bytes 3076
  40.7 4.0 copy-start.27
  42.0 5.1 copy-start.4
  44.6 16.6 %copy-start.15 = (pred[4,512,1024]{1,2,0:T(8,128)(4,1)}, pred[4,512,1024]{1,2,0:T(8,128)(4,1)S(1)}, u32[]{:S(2)}) copy-start(pred[4,512,1024]{1,2,0:T(8,128)(4,1)S(1)} %compare_and_fusion) | copy-start | bytes 6291460
  55.5 5.8 copy-start.11
  82.7 35.6 %copy-start.54 = (f32[640]{0:T(1024)S(1)}, f32[640]{0:T(1024)}, u32[]{:S(2)}) copy-start(f32[640]{0:T(1024)} %param.26) | copy-start | bytes 7684
  82.7 93.0 %all-reduce.22.cloned.1.call-start = ((), (), s32[]{:S(2)}) async-start(), calls=%async_computation.1 | async-start | bytes 10485760 | tf_op jit(solution)/shard_map/psum | solution.py:245
  115.3 4.0 copy-start.10
  119.3 7.1 copy-start.55
  130.4 7.2 copy-start.69
  130.4 9.2 %copy-start.63 = (bf16[1024,640]{1,0:T(8,128)(2,1)S(1)}, bf16[1024,640]{1,0:T(8,128)(2,1)}, u32[]{:S(2)}) copy-start(bf16[1024,640]{1,0:T(8,128)(2,1)} %param.30) | copy-start | bytes 3932164
  144.7 34.1 %copy-start.52 = (f32[640]{0:T(1024)S(1)}, f32[640]{0:T(1024)}, u32[]{:S(2)}) copy-start(f32[640]{0:T(1024)} %param.31) | copy-start | bytes 7684
  144.7 102.8 %all-reduce.24.cloned.1.call-start = ((), (), s32[]{:S(2)}) async-start(), calls=%async_computation.2 | async-start | bytes 10485760 | tf_op jit(solution)/shard_map/psum | solution.py:265
  175.7 8.1 %slice-start.4 = ((s8[5242880]{0:T(1024)(128)(4,1)}), s8[4194304]{0:T(1024)(128)(4,1)S(1)}, s32[]{:S(2)}) async-start(s8[5242880]{0:T(1024)(128)(4,1)} %bitcast.213), calls=%async_computation.9 | async-start | bytes 8388608
  178.8 5.0 slice-start.5
  183.8 23.6 %slice-start.6 = ((s8[5242880]{0:T(1024)(128)(4,1)}), s8[4194304]{0:T(1024)(128)(4,1)S(1)}, s32[]{:S(2)}) async-start(s8[5242880]{0:T(1024)(128)(4,1)} %bitcast.215), calls=%async_computation.11 | async-start | bytes 8388608
  186.4 15.7 %copy-start.24 = (bf16[2048,640]{1,0:T(8,128)(2,1)}, bf16[2048,640]{1,0:T(8,128)(2,1)S(1)}, u32[]{:S(2)}) copy-start(bf16[2048,640]{1,0:T(8,128)(2,1)S(1)} %multiply_convert_fusion.3) | copy-start | bytes 7864324
  186.4 15.7 %copy-start.66 = (bf16[640,1024]{1,0:T(8,128)(2,1)S(1)}, bf16[640,1024]{1,0:T(8,128)(2,1)}, u32[]{:S(2)}) copy-start(bf16[640,1024]{1,0:T(8,128)(2,1)} %param.28) | copy-start | bytes 3932164
  186.4 21.0 %slice-start.7 = ((s8[5242880]{0:T(1024)(128)(4,1)}), s8[1048576]{0:T(1024)(128)(4,1)S(1)}, s32[]{:S(2)}) async-start(s8[5242880]{0:T(1024)(128)(4,1)} %bitcast.215), calls=%async_computation.12 | async-start | bytes 2097152
  216.5 37.5 %slice-start.8 = ((s8[5242880]{0:T(1024)(128)(4,1)}), s8[1048576]{0:T(1024)(128)(4,1)S(1)}, s32[]{:S(2)}) async-start(s8[5242880]{0:T(1024)(128)(4,1)} %bitcast.217), calls=%async_computation.13 | async-start | bytes 2097152
  216.5 190.0 %all-reduce.28.cloned.1.call-start = ((), (), s32[]{:S(2)}) async-start(), calls=%async_computation.4 | async-start | bytes 13107200 | tf_op jit(solution)/shard_map/psum | solution.py:311
  247.5 6.7 slice-start.9
  254.2 3.7 copy-start.40
  266.5 16.3 %copy-start.17 = (bf16[4,512,2,256]{1,3,2,0:T(8,128)(2,1)}, bf16[4,512,2,256]{1,3,2,0:T(8,128)(2,1)S(1)}, u32[]{:S(2)}) copy-start(bf16[4,512,2,256]{1,3,2,0:T(8,128)(2,1)S(1)} %copy.77) | copy-start | bytes 6291460
  266.5 3.7 copy-start.16
  266.5 3.9 copy-start.35
  266.5 4.2 copy-start.36
  270.7 12.1 %copy-start.28 = (bf16[2048,1,128]{2,0,1:T(8,128)(2,1)S(1)}, bf16[2048,1,128]{2,0,1:T(8,128)(2,1)}, u32[]{:S(2)}) copy-start(bf16[2048,1,128]{2,0,1:T(8,128)(2,1)} %get-tuple-element.94) | copy-start | bytes 1572868
  270.7 12.1 %copy-start.29 = (bf16[2048,1,128]{2,0,1:T(8,128)(2,1)S(1)}, bf16[2048,1,128]{2,0,1:T(8,128)(2,1)}, u32[]{:S(2)}) copy-start(bf16[2048,1,128]{2,0,1:T(8,128)(2,1)} %get-tuple-element.95) | copy-start | bytes 1572868
  282.8 8.2 %copy-start.37 = (bf16[2048,2,128]{2,0,1:T(8,128)(2,1)S(1)}, bf16[2048,2,128]{2,0,1:T(8,128)(2,1)}, u32[]{:S(2)}) copy-start(bf16[2048,2,128]{2,0,1:T(8,128)(2,1)} %get-tuple-element.86) | copy-start | bytes 3145732
  282.8 8.2 %copy-start.38 = (bf16[2048,2,128]{2,0,1:T(8,128)(2,1)S(1)}, bf16[2048,2,128]{2,0,1:T(8,128)(2,1)}, u32[]{:S(2)}) copy-start(bf16[2048,2,128]{2,0,1:T(8,128)(2,1)} %get-tuple-element.87) | copy-start | bytes 3145732
  282.8 16.1 %slice-start.12 = ((s8[16777216]{0:T(1024)(128)(4,1)}), s8[4194304]{0:T(1024)(128)(4,1)S(1)}, s32[]{:S(2)}) async-start(s8[16777216]{0:T(1024)(128)(4,1)} %bitcast.221), calls=%async_computation.17 | async-start | bytes 8388608
  282.8 16.1 %slice-start.13 = ((s8[16777216]{0:T(1024)(128)(4,1)}), s8[4194304]{0:T(1024)(128)(4,1)S(1)}, s32[]{:S(2)}) async-start(s8[16777216]{0:T(1024)(128)(4,1)} %bitcast.221), calls=%async_computation.18 | async-start | bytes 8388608
  291.1 7.9 %slice-start.14 = ((s8[16777216]{0:T(1024)(128)(4,1)}), s8[4194304]{0:T(1024)(128)(4,1)S(1)}, s32[]{:S(2)}) async-start(s8[16777216]{0:T(1024)(128)(4,1)} %bitcast.221), calls=%async_computation.19 | async-start | bytes 8388608
  291.1 7.9 %slice-start.15 = ((s8[16777216]{0:T(1024)(128)(4,1)}), s8[4194304]{0:T(1024)(128)(4,1)S(1)}, s32[]{:S(2)}) async-start(s8[16777216]{0:T(1024)(128)(4,1)} %bitcast.221), calls=%async_computation.20 | async-start | bytes 8388608
  308.8 6.6 copy-start.7
  308.8 6.6 copy-start.47
  308.9 6.6 copy-start.57
  322.2 5.4 copy-start.14
  322.2 5.4 copy-start.18
  338.7 5.9 slice-start.2
  340.9 3.7 slice-start.3
  340.9 3.8 slice-start.10
  341.0 3.9 slice-start.11
  341.3 3.7 copy-start.34
  341.3 3.7 copy-start.43
  350.6 398.1 %all-reduce.26.cloned.1.call-start = ((), (), s32[]{:S(2)}) async-start(), calls=%async_computation.3 | async-start | bytes 23592960
  409.7 6.1 copy-start.32
  415.8 343.7 %copy-start.1 = (bf16[640,1024]{1,0:T(8,128)(2,1)S(1)}, bf16[640,1024]{1,0:T(8,128)(2,1)}, u32[]{:S(2)}) copy-start(bf16[640,1024]{1,0:T(8,128)(2,1)} %param.29) | copy-start | bytes 3932164
  748.6 10.0 %copy-start.41 = (f32[640,256]{1,0:T(8,128)S(1)}, f32[640,256]{1,0:T(8,128)}, u32[]{:S(2)}) copy-start(f32[640,256]{1,0:T(8,128)} %get-tuple-element.118) | copy-start | bytes 1966084
  (27 other events, 68.8 us)
Sparse Core Ops, SparseCore 0:
  82.8 32.3 all-reduce.19
  144.8 30.8 all-reduce.21
  216.6 30.8 all-reduce.23
  350.7 34.2 all-reduce.27
  406.6 341.9 all-reduce.25
